TPU v7x, 128 devices: a whole 4x4x4 slice. The times are simulated.
128 devices in a mesh: row: 8 (over y, z_lo), col: 16 (over x, z_hi, core).
Axes of the slice: x: 4, y: 4, z: 4 (z_hi: 2, z_lo: 2; z = z_hi * 2 + z_lo), core: 2. Of those that a mesh axis runs over, the one named last changes fastest.
Arguments:
- view_one: bfloat16 [4096, 8192], P('row', 'col'), may hold values from -6 to 6
- view_two: bfloat16 [4096, 8192], P('row', 'col'), may hold values from -6 to 6
- pair_weights: bfloat16 [8192, 8192], P('row', 'col'), may hold values from 0.25 to 2.5
Outputs:
- first_grad: bfloat16 [4096, 8192], P('row', 'col')
- second_grad: bfloat16 [4096, 8192], P('row', 'col')
All inputs are finite; a program needn't handle non-finite values.
Results may differ from a plain program's by a relative error of at most 0.004.
Values may be sent and summed in bfloat16 or wider, within the bound.
A program may use at most 128 MiB of HBM per device.

v0:
```python
import jax
import jax.numpy as jnp
from jax import lax
from jax.sharding import Mesh
from jax.sharding import PartitionSpec as P

ROW = ("row_0", "row_1")


def whole_of(array, axes, dim):
    filled = array
    for number in range(len(axes) - 1, -1, -1):
        filled = lax.all_gather(filled, axes[number], axis=dim, tiled=True)
    return filled


def per_device(view_one, view_two, pair_weights):
    wide_two = lax.all_gather(view_two, "col", axis=1, tiled=True)
    samples = view_one.shape[0] * lax.axis_size(ROW)
    local_rows = pair_weights.shape[0]
    local_cols = pair_weights.shape[1]
    regrouped = lax.all_to_all(wide_two, ROW, split_axis=1, concat_axis=0, tiled=True)
    summed = lax.dot_general(
        regrouped,
        lax.all_gather(view_one, ROW, axis=0, tiled=True),
        (((0,), (0,)), ((), ())),
        preferred_element_type=jnp.float32,
    )
    correlation = summed / samples
    row_ids = lax.axis_index(ROW) * local_rows + lax.broadcasted_iota(
        jnp.int32, (local_rows, local_cols), 0
    )
    col_ids = lax.axis_index("col") * local_cols + lax.broadcasted_iota(
        jnp.int32, (local_rows, local_cols), 1
    )
    identity = jnp.where(row_ids == col_ids, 1.0, 0.0).astype(jnp.float32)
    weighted = (pair_weights.astype(jnp.float32) * (correlation - identity)).astype(jnp.bfloat16)
    grad_cols = whole_of(weighted, ROW, 0)
    first_grad = jnp.dot(wide_two, grad_cols, preferred_element_type=jnp.float32).astype(
        jnp.bfloat16
    )
    second_flipped = lax.psum_scatter(
        lax.dot_general(
            grad_cols, view_one, (((1,), (1,)), ((), ())), preferred_element_type=jnp.float32
        ),
        "col",
        scatter_dimension=0,
        tiled=True,
    )
    return (first_grad, second_flipped.T.astype(jnp.bfloat16))


def solution(mesh):
    torus = Mesh(mesh.devices.reshape(4, 2, mesh.shape["col"]), ("row_0", "row_1", "col"))
    placed = (P(ROW, "col"), P(ROW, "col"), P(ROW, "col"))
    return jax.shard_map(
        per_device,
        mesh=torus,
        in_specs=placed,
        out_specs=(P(ROW, "col"), P(ROW, "col")),
        check_vma=False,
    )
```

profile of v0, /device:TPU:0, one launch (start us, length us, event | category | flops | bytes accessed | tf_op | source)
XLA Modules:
  0.0 564.2 jit_solution(15220778001072842064)
XLA Ops:
  8.0 0.0 all-gather.5.cloned.1.call-start
  8.0 2.0 copy.9
  10.1 0.0 all-gather.5.cloned.1.call-update
  10.1 77.0 %all-gather.5.cloned.1.call-done = bf16[512,8192]{0,1:T(8,128)(2,1)} async-done(((bf16[512,512]{0,1:T(8,128)(2,1)}), bf16[512,8192]{0,1:T(8,128)(2,1)}) %all-gather.5.cloned.1.call-update) | async-done | bytes 8388624 | tf_op jit(solution)/shard_map/all_gather | solution.py:18
  87.1 5.0 all-to-all-start
  92.1 0.0 all-gather.7.cloned.1.call-start
  92.2 0.5 all-gather.7.cloned.1.call-update
  92.7 0.0 all-gather.9.cloned.1.call-start
  92.8 125.2 %all-to-all-done = bf16[512,8,1024]{0,2,1:T(8,128)(2,1)} async-done(((bf16[512,8,1024]{0,2,1:T(8,128)(2,1)}), bf16[512,8,1024]{0,2,1:T(8,128)(2,1)}, u32[]{:S(2)}, u32[]{:S(2)}) %all-to-all-start) | async-done | bytes 8388640 | tf_op jit(solution)/shard_map/all_to_all | solution.py:22
  218.0 0.0 copy-start.1
  218.0 11.6 %copy.10 = bf16[8,512,1024]{2,1,0:T(8,128)(2,1)} copy(bf16[8,512,1024]{1,2,0:T(8,128)(2,1)} %bitcast.1) | data formatting | bytes 16777216 | tf_op jit(solution)/shard_map/all_to_all | solution.py:22
  229.6 34.8 %all-gather.7.cloned.1.call-done = bf16[4096,512]{1,0:T(8,128)(2,1)} async-done(((bf16[512,512]{1,0:T(8,128)(2,1)}), bf16[4096,512]{1,0:T(8,128)(2,1)}) %all-gather.7.cloned.1.call-update) | async-done | bytes 4194320 | tf_op jit(solution)/shard_map/all_gather | solution.py:25
  264.4 0.0 copy-done.1
  264.4 0.0 copy-start
  264.4 10.4 %multiply_convert_fusion = bf16[1024,512]{1,0:T(8,128)(2,1)} fusion(bf16[1024,512]{1,0:T(8,128)(2,1)S(1)} %copy-done.1, bf16[4096,1024]{1,0:T(8,128)(2,1)} %bitcast.14, bf16[4096,512]{1,0:T(8,128)(2,1)} %all-gather.7.cloned.1.call-done, s32[512]{0:T(512)S(1)} %iota_add_fusion.1, s32[1024]{0:T(1024)S(1)} %iota_add_fusion), kind=kOutput, calls=%fused_computation | convolution fusion | flops 4298637312 | bytes 14686208 | tf_op jit(solution)/shard_map/dot_general | solution.py:23
  274.8 0.0 all-gather.9.cloned.1.call-update
  274.8 0.0 all-gather.11.cloned.1.call-start
  274.8 34.0 %all-gather.9.cloned.1.call-done = bf16[2048,512]{1,0:T(8,128)(2,1)} async-done(((bf16[1024,512]{1,0:T(8,128)(2,1)}), bf16[2048,512]{1,0:T(8,128)(2,1)}) %all-gather.9.cloned.1.call-update) | async-done | bytes 2097168 | tf_op jit(solution)/shard_map/all_gather | solution.py:13
  308.8 0.0 all-gather.11.cloned.1.call-update
  308.8 0.0 reduce-scatter.2.cloned.1.call-start
  308.9 85.4 %all-gather.11.cloned.1.call-done = bf16[8192,512]{1,0:T(8,128)(2,1)} async-done(((bf16[2048,512]{1,0:T(8,128)(2,1)}), bf16[8192,512]{1,0:T(8,128)(2,1)}) %all-gather.11.cloned.1.call-update) | async-done | bytes 8388624 | tf_op jit(solution)/shard_map/all_gather | solution.py:13
  394.3 0.0 copy-done
  394.3 11.7 %fusion.1 = f32[8192,512]{1,0:T(8,128)} fusion(bf16[8192,512]{1,0:T(8,128)(2,1)} %all-gather.11.cloned.1.call-done, bf16[512,512]{1,0:T(8,128)(2,1)S(1)} %copy-done), kind=kOutput, calls=%fused_computation.6 | convolution fusion | flops 4294967296 | bytes 25690112 | tf_op jit(solution)/shard_map/dot_general | solution.py:43
  405.9 0.0 reduce-scatter.2.cloned.1.call-update
  406.0 10.3 %fusion = bf16[512,512]{0,1:T(8,128)(2,1)S(1)} fusion(bf16[8192,512]{1,0:T(8,128)(2,1)} %all-gather.11.cloned.1.call-done, bf16[512,8192]{0,1:T(8,128)(2,1)} %all-gather.5.cloned.1.call-done), kind=kOutput, calls=%fused_computation.2 | convolution fusion | flops 4295229440 | bytes 17301504 | tf_op jit(solution)/shard_map/dot_general | solution.py:39
  416.2 1.0 copy.11
  417.2 137.1 %reduce-scatter.2.cloned.1.call-done = f32[512,512]{1,0:T(8,128)} async-done(((f32[8192,512]{1,0:T(8,128)}), f32[512,512]{1,0:T(8,128)}) %reduce-scatter.2.cloned.1.call-update) | async-done | bytes 1048592 | tf_op jit(solution)/shard_map/reduce_scatter | solution.py:42
  554.3 1.3 convert_bitcast_fusion
  555.6 1.0 copy.12
  (2 shorter events, 0.0 us)
Async XLA Ops:
  8.0 79.1 %all-gather.5.cloned.1.call-start = ((), (), s32[]{:S(2)}) async-start(), calls=%async_computation.2 | async-start | bytes 8912896 | tf_op jit(solution)/shard_map/all_gather | solution.py:18
  87.1 130.9 %all-to-all-start = ((bf16[512,8,1024]{0,2,1:T(8,128)(2,1)}), bf16[512,8,1024]{0,2,1:T(8,128)(2,1)}, u32[]{:S(2)}, u32[]{:S(2)}) async-start(bf16[512,8,1024]{0,2,1:T(8,128)(2,1)} %bitcast.13), calls=%async_computation | async-start | bytes 16777216 | tf_op jit(solution)/shard_map/all_to_all | solution.py:22
  92.1 172.3 %all-gather.7.cloned.1.call-start = ((), (), s32[]{:S(2)}) async-start(), calls=%async_computation.3 | async-start | bytes 4718592 | tf_op jit(solution)/shard_map/all_gather | solution.py:25
  92.7 216.1 %all-gather.9.cloned.1.call-start = ((), (), s32[]{:S(2)}) async-start(), calls=%async_computation.4 | async-start | bytes 3145728 | tf_op jit(solution)/shard_map/all_gather | solution.py:13
  218.0 46.4 %copy-start.1 = (bf16[1024,512]{1,0:T(8,128)(2,1)S(1)}, bf16[1024,512]{1,0:T(8,128)(2,1)}, u32[]{:S(2)}) copy-start(bf16[1024,512]{1,0:T(8,128)(2,1)} %param.5) | copy-start | bytes 3145732
  264.4 129.9 %copy-start = (bf16[512,512]{1,0:T(8,128)(2,1)S(1)}, bf16[512,512]{1,0:T(8,128)(2,1)}, u32[]{:S(2)}) copy-start(bf16[512,512]{1,0:T(8,128)(2,1)} %param.3) | copy-start | bytes 1572868
  274.8 119.5 %all-gather.11.cloned.1.call-start = ((), (), s32[]{:S(2)}) async-start(), calls=%async_computation.5 | async-start | bytes 10485760 | tf_op jit(solution)/shard_map/all_gather | solution.py:13
  308.8 245.5 %reduce-scatter.2.cloned.1.call-start = ((), (), s32[]{:S(2)}) async-start(), calls=%async_computation.6 | async-start | bytes 17825792 | tf_op jit(solution)/shard_map/reduce_scatter | solution.py:42
Sparse Core Ops, SparseCore 0:
  11.8 75.2 all-gather.4
  406.1 148.1 reduce-scatter.1
Sparse Core Ops, SparseCore 1:
  94.2 170.1 all-gather.6
  274.9 33.9 all-gather.8
  310.3 83.9 all-gather.10
where the time goes:
time: 565 us; the launch traced here: 564 us
  waiting for transfers between devices  494 us (87%)
  matrix products  32.3 us (6%)
  local copies, waits for them, and re-layouts  15.7 us (3%)
  between operations  15.7 us (3%)
    reduce_scatter x1, waiting for transfers between devices, per_device(): lax.psum_scatter(lax.dot_general(grad_cols, view_one, (((1,), (1,)), ((),...  137 us
    all_to_all x1, waiting for transfers between devices, per_device(): lax.all_to_all(wide_two, ROW, split_axis=1, concat_axis=0, tiled=True)  125 us
    all_gather x2, waiting for transfers between devices, whole_of(): filled = lax.all_gather(filled, axes[number], axis=dim, tiled=True)  119 us
    all_gather x1, waiting for transfers between devices, per_device(): wide_two = lax.all_gather(view_two, 'col', axis=1, tiled=True)  77 us
    all_gather x1, waiting for transfers between devices, per_device(): lax.all_gather(view_one, ROW, axis=0, tiled=True)  34.8 us
    dot_general x1, matrix products, per_device(): lax.dot_general(grad_cols, view_one, (((1,), (1,)), ((), ())), preferred_...  11.7 us
    all_to_all x1, local copies, waits for them, and re-layouts, per_device(): lax.all_to_all(wide_two, ROW, split_axis=1, concat_axis=0, tiled=True)  11.6 us
  transfers between devices with their start and end apart: 6, of which 6 were waited for; matrix products, arithmetic and copies ran while one was open for 4% of the time, Pallas kernels for 0%

commit v1 on v0

v1 whole, which is shorter than its diff:
```python
import functools

import jax
import jax.numpy as jnp
from jax import lax
from jax.experimental import pallas as pl
from jax.experimental.pallas import tpu as pltpu
from jax.sharding import PartitionSpec as P

ROUNDS = 2
PIECES = 2 * ROUNDS
F32 = jnp.float32
BF16 = jnp.bfloat16


def kernel(
    v1, v2, w, o1, o2,
    z1o, z1p, z2o, z2p, acc, go, gp, gr, p1, p2, rx2, rx1, rz, ry2, ry1, rzl, fin,
    lsem, ssem, k1s, k2s, zls, y1s, y2s, ts, us, x1s, x2s, gs, sx2, sx1, sz, sy2, sy1, szl, sfin,
):
    n = PIECES
    row, col = lax.axis_index("row"), lax.axis_index("col")
    y, zl = row // 2, row % 2
    x, zh, k = col // 4, (col // 2) % 2, col % 2
    samples = v1.shape[0] * v1.shape[1] * 8

    def dev(x=x, y=y, zh=zh, zl=zl, k=k):
        return (y * 2 + zl, x * 4 + zh * 2 + k)

    def mod4(a):
        return (a + 8) % 4

    xr, xl, yr, yl = mod4(x + 1), mod4(x - 1), mod4(y + 1), mod4(y - 1)
    d = mod4(x - y)
    moved = d != 0
    crossed = zh != zl
    t_dest = dev(x=mod4(x + d), y=mod4(y + d))
    t_source = dev(x=mod4(x - d), y=mod4(y - d))
    partner = dev(k=1 - k)

    started = []

    def send(src, dst, recv, where, cond=None):
        number = len(started)
        copy = pltpu.make_async_remote_copy(
            src_ref=src, dst_ref=dst, send_sem=ssem.at[number], recv_sem=recv,
            device_id=where, device_id_type=pl.DeviceIdType.MESH,
        )
        started.append((copy, cond))
        if cond is None:
            copy.start()
        else:
            pl.when(cond)(copy.start)

    def arrived(dst, recv, cond=None):
        copy = pltpu.make_async_remote_copy(
            src_ref=dst, dst_ref=dst, send_sem=ssem.at[0], recv_sem=recv,
            device_id=partner, device_id_type=pl.DeviceIdType.MESH,
        )
        if cond is None:
            copy.wait_recv()
        else:
            pl.when(cond)(copy.wait_recv)

    def slot1(yy, zz):
        return (yy * 2 + zz) * n

    def home(xx):
        return mod4(2 * y - xx)

    own = slot1(y, zl)
    load = pltpu.make_async_copy(v1, z1o.at[pl.ds(own, n)], lsem.at[0])
    load.start()
    barrier = pltpu.get_barrier_semaphore()
    for where in (
        dev(x=xr), dev(x=xl), dev(y=yr), dev(y=yl), partner,
        dev(zl=1 - zl), dev(zh=1 - zh), dev(zh=1 - zh, zl=1 - zl),
    ):
        pl.semaphore_signal(barrier, inc=1, device_id=where, device_id_type=pl.DeviceIdType.MESH)

    @pl.when(moved)
    def _():
        pl.semaphore_signal(barrier, inc=1, device_id=t_dest, device_id_type=pl.DeviceIdType.MESH)
        pl.semaphore_signal(barrier, inc=1, device_id=t_source, device_id_type=pl.DeviceIdType.MESH)

    pl.semaphore_wait(barrier, jnp.where(moved, 10, 8))

    def landing(yy):
        return jnp.where(crossed, 8 * n, slot1(yy, zl))

    first = landing(home(x))
    for piece in range(n):
        send(v2.at[piece], z2o.at[landing(y) + piece], ts.at[piece], t_dest, moved)

        @pl.when(d == 0)
        def _():
            pltpu.make_async_copy(v2.at[piece], z2o.at[first + piece], ts.at[piece]).start()

    load.wait()
    send(z1o.at[pl.ds(own, n)], z1o.at[pl.ds(own, n)], zls.at[0], dev(zl=1 - zl))
    for piece in range(n):
        send(z1o.at[own + piece], z1p.at[own + piece], k1s.at[own + piece], partner)

    def z_move(piece):
        arrived(z2o.at[first + piece], ts.at[piece], moved)

        @pl.when(d == 0)
        def _():
            pltpu.make_async_copy(v2.at[piece], z2o.at[first + piece], ts.at[piece]).wait()

        there = slot1(home(x), zl) + piece
        send(z2o.at[first + piece], z2o.at[there], us.at[zl, piece], dev(zh=1 - zl, zl=zh))
        send(z2o.at[first + piece], z2o.at[there], us.at[zl, piece], dev(zh=zl, zl=zh), crossed)

    def y_spread(zz, number):
        there = slot1(y, zz)
        block = z1o.at[pl.ds(there, n)]
        send(block, block, y1s.at[0, number], dev(y=yr))
        send(block, block, y1s.at[1, number], dev(y=yl))

    for piece in range(n):
        z_move(piece)
    y_spread(zl, 0)
    there = slot1(y, 1 - zl)
    arrived(z1o.at[pl.ds(there, n)], zls.at[0])
    y_spread(1 - zl, 1)
    for piece in range(n):
        send(z1o.at[there + piece], z1p.at[there + piece], k1s.at[there + piece], partner)

    def x_spread(zz, piece):
        there = slot1(home(x), zz) + piece
        arrived(z2o.at[there], us.at[zz, piece], jnp.logical_or(crossed, zl != zz))
        send(z2o.at[there], z2o.at[there], x1s.at[0, zz, piece], dev(x=xr))
        send(z2o.at[there], z2o.at[there], x1s.at[1, zz, piece], dev(x=xl))
        send(z2o.at[there], z2p.at[there], k2s.at[there], partner)

    for piece in range(n):
        for zz in range(2):
            x_spread(zz, piece)

    def y_forward(number):
        zz = zl if number == 0 else 1 - zl
        for side, (source, target) in enumerate(((yl, yr), (yr, yl))):
            there = slot1(source, zz)
            block = z1o.at[pl.ds(there, n)]
            arrived(block, y1s.at[side, number])
            for half in range(ROUNDS):
                piece = z1o.at[there + 2 * half + side]
                send(piece, piece, y2s.at[side, number, half], dev(y=target))
            for piece in range(n):
                send(z1o.at[there + piece], z1p.at[there + piece], k1s.at[there + piece], partner)

    def x_forward(zz, piece):
        for side, (source, target) in enumerate(((xl, xr), (xr, xl))):
            there = slot1(home(source), zz) + piece
            arrived(z2o.at[there], x1s.at[side, zz, piece])
            if piece % 2 == side:
                send(z2o.at[there], z2o.at[there], x2s.at[zz, piece], dev(x=target))
            send(z2o.at[there], z2p.at[there], k2s.at[there], partner)

    y_forward(0)
    for piece in range(n):
        if piece == n // 2:
            y_forward(1)
        for zz in range(2):
            x_forward(zz, piece)
    for number in range(2):
        zz = zl if number == 0 else 1 - zl
        there = slot1(mod4(y + 2), zz)
        for half in range(ROUNDS):
            for side in range(2):
                piece = there + 2 * half + side
                arrived(z1o.at[piece], y2s.at[side, number, half])
                send(z1o.at[piece], z1p.at[piece], k1s.at[piece], partner)

    acc[...] = jnp.zeros_like(acc)
    rows = v1.shape[0] * v1.shape[1]
    depth = v1.shape[2]
    tile = min(256, depth)

    def correlate(yy, zz):
        there = slot1(yy, zz)
        for piece in range(n):
            arrived(z2p.at[there + piece], k2s.at[there + piece])
        right = z1o[pl.ds(there, n)].reshape(rows, depth)
        for part, held in enumerate((z2o, z2p)):
            for start in range(0, depth, tile):
                left = held[pl.ds(there, n), :, pl.ds(start, tile)].reshape(rows, tile)
                acc[part, pl.ds(start, tile), :] += lax.dot_general(
                    left, right, (((0,), (0,)), ((), ())), preferred_element_type=F32
                )

    def near(step, carry):
        correlate(home(mod4(x + 3 * (step // 2 == 1) + (step // 2 == 2))), step % 2)
        return carry

    lax.fori_loop(0, 6, near, 0)
    for piece in range(n):
        for zz in range(2):
            there = slot1(home(mod4(x + 2)), zz) + piece
            arrived(z2o.at[there], x2s.at[zz, piece])
            send(z2o.at[there], z2p.at[there], k2s.at[there], partner)

    def far(step, carry):
        correlate(home(mod4(x + 2)), step)
        return carry

    lax.fori_loop(0, 2, far, 0)

    def weigh(part, target):
        half = k if part == 0 else 1 - k
        for start in range(0, depth, tile):
            shape = (tile, depth)
            row_ids = row * (2 * depth) + half * depth + start + lax.broadcasted_iota(jnp.int32, shape, 0)
            col_ids = col * depth + lax.broadcasted_iota(jnp.int32, shape, 1)
            identity = jnp.where(row_ids == col_ids, 1.0, 0.0).astype(F32)
            correlation = acc[part, pl.ds(start, tile), :] / samples
            weights = w[half, pl.ds(start, tile), :].astype(F32)
            target[pl.ds(start, tile), :] = (weights * (correlation - identity)).astype(BF16)

    weigh(1, gp)
    send(gp, gr, gs.at[0], partner)
    weigh(0, go)

    def first_part(there):
        p1[there] = (
            jnp.dot(z2o[there], go[...], preferred_element_type=F32)
            + jnp.dot(z2p[there], gp[...], preferred_element_type=F32)
        ).astype(BF16)

    turned = (((1,), (1,)), ((), ()))

    def second_part(there):
        p2[there] = (
            lax.dot_general(z1o[there], go[...], turned, preferred_element_type=F32)
            + lax.dot_general(z1p[there], gr[...], turned, preferred_element_type=F32)
        ).astype(BF16)

    def over(base, count, part):
        def body(step, carry):
            part(base(step))
            return carry

        lax.fori_loop(0, count, body, 0)

    y_far, x_far = mod4(y + 2), home(mod4(x + 2))
    over(lambda step: slot1(y_far, 0) + step, 2 * n, first_part)
    for piece in range(n):
        for zz in range(2):
            send(p1.at[slot1(y_far, zz) + piece], ry2.at[zz, piece], sy2.at[zz, piece], dev(y=yr if piece % 2 == 0 else yl))
    arrived(gr, gs.at[0])

    def all_of_z1p(step, carry):
        arrived(z1p.at[step], k1s.at[step])
        return carry

    lax.fori_loop(0, 8 * n, all_of_z1p, 0)
    over(lambda step: slot1(x_far, 0) + step, 2 * n, second_part)
    for piece in range(n):
        for zz in range(2):
            send(p2.at[slot1(x_far, zz) + piece], rx2.at[zz, piece], sx2.at[zz, piece], dev(x=xr if piece % 2 == 0 else xl))

    def around(base, here):
        def at(step):
            block = step // (2 * n)
            return base(mod4(here + (block == 0) + 3 * (block == 1))) + step % (2 * n)

        return at

    over(around(lambda xx: slot1(home(xx), 0), x), 6 * n, second_part)
    over(around(lambda yy: slot1(yy, 0), y), 6 * n, first_part)

    def pass_on(held, far_in, far_sem, near_in, near_sem, base, zz, piece, targets):
        for side, (ahead, where) in enumerate(targets):
            there = base(ahead, zz) + piece
            if piece % 2 == side:
                arrived(far_in.at[zz, piece], far_sem.at[zz, piece])
                held[there] = (held[there].astype(F32) + far_in[zz, piece].astype(F32)).astype(BF16)
            send(held.at[there], near_in.at[side, zz, piece], near_sem.at[side, zz, piece], where)

    x_targets = ((xr, dev(x=xr)), (xl, dev(x=xl)))
    y_targets = ((yr, dev(y=yr)), (yl, dev(y=yl)))
    for piece in range(n):
        for zz in range(2):
            pass_on(p2, rx2, sx2, rx1, sx1, lambda xx, zz: slot1(home(xx), zz), zz, piece, x_targets)
            pass_on(p1, ry2, sy2, ry1, sy1, slot1, zz, piece, y_targets)

    def total(held, there, near_in, near_sem, zz, piece):
        for side in range(2):
            arrived(near_in.at[side, zz, piece], near_sem.at[side, zz, piece])
        return held[there].astype(F32) + near_in[0, zz, piece].astype(F32) + near_in[1, zz, piece].astype(F32)

    for piece in range(n):
        for zz in range(2):
            there = slot1(home(x), zz) + piece
            value = total(p2, there, rx1, sx1, zz, piece).astype(BF16)
            stays = jnp.logical_and(zl == zh, zl == zz)
            p2[there] = value
            send(
                p2.at[there], rz.at[zh, piece], sz.at[zh, piece], dev(zh=zl, zl=zz), jnp.logical_not(stays)
            )

            @pl.when(stays)
            def _():
                rz[zh, piece] = value

        there = slot1(y, 0) + (1 - zl) * n + piece
        for zz in range(2):
            @pl.when(zz != zl)
            def _():
                p1[slot1(y, zz) + piece] = total(p1, slot1(y, zz) + piece, ry1, sy1, zz, piece).astype(BF16)

        send(p1.at[there], rzl.at[piece], szl.at[piece], dev(zl=1 - zl))

    for piece in range(n):
        for source in range(2):
            arrived(rz.at[source, piece], sz.at[source, piece], jnp.logical_or(crossed, zh != source))
        value = (rz[0, piece].astype(F32) + rz[1, piece].astype(F32)).astype(BF16)
        there = slot1(home(x), 0) + piece
        o2[piece] = value
        fin[0, piece] = value
        send(fin.at[0, piece], fin.at[1, piece], sfin.at[piece], t_source, moved)

    for piece in range(n):
        arrived(rzl.at[piece], szl.at[piece])
        for zz in range(2):
            @pl.when(zz == zl)
            def _():
                value = total(p1, slot1(y, zz) + piece, ry1, sy1, zz, piece)
                o1[piece] = (value + rzl[piece].astype(F32)).astype(BF16)

    for piece in range(n):
        arrived(fin.at[1, piece], sfin.at[piece], moved)

        @pl.when(moved)
        def _():
            o2[piece] = fin[1, piece]

    for copy, cond in started:
        if cond is None:
            copy.wait_send()
        else:
            pl.when(cond)(copy.wait_send)


def per_device(view_one, view_two, pair_weights):
    n = PIECES
    rows, depth = view_one.shape
    piece = (rows // n, depth)
    vmem = lambda *lead: pltpu.VMEM(lead + piece, BF16)
    square = (depth, depth)
    dma = lambda *shape: pltpu.SemaphoreType.DMA(shape)
    cut = (n,) + piece
    flops = 2 * 3 * 8 * rows * 2 * depth * depth
    first, second = pl.pallas_call(
        kernel,
        out_shape=[jax.ShapeDtypeStruct(cut, BF16)] * 2,
        in_specs=[
            pl.BlockSpec(memory_space=pltpu.HBM),
            pl.BlockSpec(memory_space=pltpu.HBM),
            pl.BlockSpec(memory_space=pltpu.VMEM),
        ],
        out_specs=[pl.BlockSpec(memory_space=pltpu.VMEM)] * 2,
        scratch_shapes=[
            vmem(8 * n), vmem(8 * n), vmem(9 * n), vmem(8 * n),
            pltpu.VMEM((2,) + square, F32),
            pltpu.VMEM(square, BF16), pltpu.VMEM(square, BF16), pltpu.VMEM(square, BF16),
            vmem(8 * n), vmem(8 * n),
            vmem(2, n), vmem(2, 2, n), vmem(2, n),
            vmem(2, n), vmem(2, 2, n), vmem(n), vmem(2, n),
            dma(1), dma(SENDS), dma(8 * n), dma(8 * n), dma(1), dma(2, 2), dma(2, 2, ROUNDS),
            dma(n), dma(2, n), dma(2, 2, n), dma(2, n), dma(1),
            dma(2, n), dma(2, 2, n), dma(2, n), dma(2, n), dma(2, 2, n), dma(n), dma(n),
        ],
        compiler_params=pltpu.CompilerParams(
            collective_id=0, has_side_effects=True, vmem_limit_bytes=60 * 1024 * 1024
        ),
        cost_estimate=pl.CostEstimate(flops=flops, bytes_accessed=8 * rows * depth, transcendentals=0),
    )(view_one.reshape(cut), view_two.reshape(cut), pair_weights.reshape((2,) + square))
    return first.reshape(rows, depth), second.reshape(rows, depth)


SENDS = 60 * PIECES


def solution(mesh):
    placed = (P("row", "col"),) * 3
    return jax.shard_map(
        per_device, mesh=mesh, in_specs=placed, out_specs=(P("row", "col"),) * 2, check_vma=False
    )
```

time: 565 us -> 149 us (0.26)
  the two profiles are of different devices: /device:TPU:0 before, /device:TPU:9 now
where the time goes in v1:
time: 149 us
  Pallas kernels  145 us (97%)
  local copies, waits for them, and re-layouts  2.72 us (2%)
    pallas_call x1, Pallas kernels, per_device(): pl.pallas_call(kernel, out_shape=[jax.ShapeDtypeStruct(cut, BF16)] * 2, i...  145 us

profile of v1, /device:TPU:9, one launch (start us, length us, event | category | flops | bytes accessed | tf_op | source)
XLA Modules:
  0.0 148.8 jit_solution(2160040114553182317)
XLA Ops:
  0.6 145.5 %shard_map.50 = (bf16[4,128,512]{2,1,0:T(8,128)(2,1)}, bf16[4,128,512]{2,1,0:T(8,128)(2,1)}) custom-call(bf16[4,128,512]{2,1,0:T(8,128)(2,1)} %bitcast.8, bf16[4,128,512]{2,1,0:T(8,128)(2,1)} %bitcast.9, bf16[2,512,512]{2,1,0:T(8,128)(2,1)} %bitcast.7), custom_call_target="tpu_custom_call" | custom-call | flops 12884901888 | bytes 2097152 | tf_op jit(solution)/shard_map/pallas_call | solution.py:355
  146.1 0.0 copy-start
  146.1 1.9 %copy.7 = bf16[512,512]{1,0:T(8,128)(2,1)} copy(bf16[512,512]{1,0:T(8,128)(2,1)} %bitcast.6) | data formatting | bytes 1048576
  148.0 0.0 copy-done
  148.0 0.8 copy.8
Async XLA Ops:
  146.1 1.9 %copy-start = (bf16[4,128,512]{2,1,0:T(8,128)(2,1)S(1)}, bf16[4,128,512]{2,1,0:T(8,128)(2,1)}, u32[]{:S(2)}) copy-start(bf16[4,128,512]{2,1,0:T(8,128)(2,1)} %get-tuple-element.5) | copy-start | bytes 1572868

commit v2 on v0

v2 whole, which is shorter than its diff:
```python
import functools

import jax
import jax.numpy as jnp
from jax import lax
from jax.experimental import pallas as pl
from jax.experimental.pallas import tpu as pltpu
from jax.sharding import PartitionSpec as P

F32 = jnp.float32
BF16 = jnp.bfloat16
PIECES = 8
CHUNKS = 4
WIDE = PIECES // CHUNKS
LAG = 2
TURNED = (((1,), (1,)), ((), ()))


def kernel(
    v1, v2, w, o1, o2,
    z1o, z1p, z2o, z2p, acc, go, gp, gr, p1, p2, rx2, rx1, rz, ry2, ry1, rzl, fin_out, fin_in,
    lsem, ssem, k1s, k2s, zls, y1s, y2s, ts, us, x1s, x2s, gs, sx2, sx1, sz, sy2, sy1, szl, sfin,
):
    row, col = lax.axis_index("row"), lax.axis_index("col")
    y, zl = row // 2, row % 2
    x, zh, k = col // 4, (col // 2) % 2, col % 2
    depth = v1.shape[2]
    samples = v1.shape[0] * v1.shape[1] * 8
    tile = min(256, depth)

    def dev(x=x, y=y, zh=zh, zl=zl, k=k):
        return (y * 2 + zl, x * 4 + zh * 2 + k)

    def mod4(a):
        return (a + 8) % 4

    xr, xl, yr, yl = mod4(x + 1), mod4(x - 1), mod4(y + 1), mod4(y - 1)
    d = mod4(x - y)
    moved = d != 0
    crossed = zh != zl
    t_dest = dev(x=mod4(x + d), y=mod4(y + d))
    t_source = dev(x=mod4(x - d), y=mod4(y - d))
    partner = dev(k=1 - k)
    x_sides = (dev(x=xr), dev(x=xl))
    y_sides = (dev(y=yr), dev(y=yl))

    started = []

    def send(src, dst, recv, where, cond=None):
        copy = pltpu.make_async_remote_copy(
            src_ref=src, dst_ref=dst, send_sem=ssem.at[len(started)], recv_sem=recv,
            device_id=where, device_id_type=pl.DeviceIdType.MESH,
        )
        started.append((copy, cond))
        if cond is None:
            copy.start()
        else:
            pl.when(cond)(copy.start)

    def arrived(dst, recv, cond=None):
        copy = pltpu.make_async_remote_copy(
            src_ref=dst, dst_ref=dst, send_sem=ssem.at[0], recv_sem=recv,
            device_id=partner, device_id_type=pl.DeviceIdType.MESH,
        )
        if cond is None:
            copy.wait_recv()
        else:
            pl.when(cond)(copy.wait_recv)

    def home(xx):
        return mod4(2 * y - xx)

    def part(chunk):
        return pl.ds(chunk * WIDE, WIDE)

    load = pltpu.make_async_copy(v1, z1o.at[y, :, zl], lsem.at[0])
    load.start()
    barrier = pltpu.get_barrier_semaphore()
    for where in x_sides + y_sides + (
        partner, dev(zl=1 - zl), dev(zh=1 - zh), dev(zh=1 - zh, zl=1 - zl),
    ):
        pl.semaphore_signal(barrier, inc=1, device_id=where, device_id_type=pl.DeviceIdType.MESH)

    @pl.when(moved)
    def _():
        pl.semaphore_signal(barrier, inc=1, device_id=t_dest, device_id_type=pl.DeviceIdType.MESH)
        pl.semaphore_signal(barrier, inc=1, device_id=t_source, device_id_type=pl.DeviceIdType.MESH)

    pl.semaphore_wait(barrier, jnp.where(moved, 10, 8))

    spare = jnp.where(crossed, 0, zl)

    def landing(yy, chunk):
        return z2o.at[jnp.where(crossed, 4, yy), part(chunk), spare]

    def local(chunk):
        return pltpu.make_async_copy(v2.at[part(chunk)], landing(home(x), chunk), ts.at[chunk])

    for chunk in range(CHUNKS):
        send(v2.at[part(chunk)], landing(y, chunk), ts.at[chunk], t_dest, moved)
        pl.when(d == 0)(local(chunk).start)

    def share1(yy, zz, chunk):
        block = z1o.at[yy, part(chunk), zz]
        send(block, z1p.at[yy, part(chunk), zz], k1s.at[yy, zz, chunk], partner)

    def share2(yy, zz, chunk):
        block = z2o.at[yy, part(chunk), zz]
        send(block, z2p.at[yy, part(chunk), zz], k2s.at[yy, zz, chunk], partner)

    load.wait()
    send(z1o.at[y, :, zl], z1o.at[y, :, zl], zls.at[0], dev(zl=1 - zl))
    for chunk in range(CHUNKS):
        share1(y, zl, chunk)

    for chunk in range(CHUNKS):
        here = landing(home(x), chunk)
        arrived(here, ts.at[chunk], moved)
        pl.when(d == 0)(local(chunk).wait)
        there = z2o.at[home(x), part(chunk), zl]
        send(here, there, us.at[zl, chunk], dev(zh=1 - zl, zl=zh))
        send(here, there, us.at[zl, chunk], dev(zh=zl, zl=zh), crossed)

    def y_spread(number, zz):
        block = z1o.at[y, :, zz]
        for side in range(2):
            send(block, block, y1s.at[side, number], y_sides[side])

    y_spread(0, zl)
    arrived(z1o.at[y, :, 1 - zl], zls.at[0])
    y_spread(1, 1 - zl)
    for chunk in range(CHUNKS):
        share1(y, 1 - zl, chunk)

    for chunk in range(CHUNKS):
        for zz in range(2):
            block = z2o.at[home(x), part(chunk), zz]
            arrived(block, us.at[zz, chunk], jnp.logical_or(crossed, zl != zz))
            for side in range(2):
                send(block, block, x1s.at[side, zz, chunk], x_sides[side])
            share2(home(x), zz, chunk)

    def y_forward(number, zz):
        for side, source in enumerate((yl, yr)):
            arrived(z1o.at[source, :, zz], y1s.at[side, number])
            for half in range(CHUNKS // 2):
                block = z1o.at[source, part(2 * half + side), zz]
                send(block, block, y2s.at[side, number, half], y_sides[side])
            for chunk in range(CHUNKS):
                share1(source, zz, chunk)

    def x_forward(zz, chunk):
        for side, source in enumerate((xl, xr)):
            block = z2o.at[home(source), part(chunk), zz]
            arrived(block, x1s.at[side, zz, chunk])
            if chunk % 2 == side:
                send(block, block, x2s.at[zz, chunk], x_sides[side])
            share2(home(source), zz, chunk)

    y_forward(0, zl)
    for chunk in range(CHUNKS):
        if chunk == CHUNKS // 2:
            y_forward(1, 1 - zl)
        for zz in range(2):
            x_forward(zz, chunk)

    def flat(ref, yy, columns=slice(None)):
        block = ref[yy, :, :, :, columns]
        return block.reshape(-1, block.shape[-1])

    def correlate(yy):
        for zz in range(2):
            for chunk in range(CHUNKS):
                arrived(z2p.at[yy, part(chunk), zz], k2s.at[yy, zz, chunk])
        right = flat(z1o, yy)
        for number, held in enumerate((z2o, z2p)):
            for start in range(0, depth, tile):
                left = flat(held, yy, pl.ds(start, tile))
                acc[number, pl.ds(start, tile), :] += lax.dot_general(
                    left, right, (((0,), (0,)), ((), ())), preferred_element_type=F32
                )

    def early(step, carry):
        first = jnp.where(d == 2, 1, 0)
        second = jnp.where(jnp.logical_or(d == 0, d == 3), 1, 3)
        correlate(home(mod4(x + jnp.where(step == 0, first, second))))
        return carry

    acc[...] = jnp.zeros_like(acc)
    lax.fori_loop(0, 2, early, 0)
    for number in range(2):
        zz = zl if number == 0 else 1 - zl
        for half in range(CHUNKS // 2):
            for side in range(2):
                chunk = 2 * half + side
                arrived(z1o.at[mod4(y + 2), part(chunk), zz], y2s.at[side, number, half])
                share1(mod4(y + 2), zz, chunk)
    for chunk in range(CHUNKS):
        for zz in range(2):
            arrived(z2o.at[home(mod4(x + 2)), part(chunk), zz], x2s.at[zz, chunk])
            share2(home(mod4(x + 2)), zz, chunk)

    def late(step, carry):
        correlate(home(mod4(x + jnp.where(step == 0, jnp.where(d == 0, 3, 2 - d), 2))))
        return carry

    lax.fori_loop(0, 2, late, 0)

    def weigh(number, target):
        half = k if number == 0 else 1 - k
        for start in range(0, depth, tile):
            shape = (tile, depth)
            row_ids = row * (2 * depth) + half * depth + start + lax.broadcasted_iota(jnp.int32, shape, 0)
            col_ids = col * depth + lax.broadcasted_iota(jnp.int32, shape, 1)
            identity = jnp.where(row_ids == col_ids, 1.0, 0.0).astype(F32)
            correlation = acc[number, pl.ds(start, tile), :] / samples
            weights = w[half, pl.ds(start, tile), :].astype(F32)
            target[pl.ds(start, tile), :] = (weights * (correlation - identity)).astype(BF16)

    weigh(1, gp)
    send(gp, gr, gs.at[0], partner)
    weigh(0, go)

    size = PIECES // 2

    def slab(ref, yy, s):
        return ref[yy, pl.ds(s * size, size)].reshape(-1, depth)

    def first_part(yy, s):
        total = jnp.dot(slab(z2o, yy, s), go[...], preferred_element_type=F32)
        total += jnp.dot(slab(z2p, yy, s), gp[...], preferred_element_type=F32)
        p1[yy, pl.ds(s * size, size)] = total.astype(BF16).reshape((size,) + p1.shape[2:])

    def second_part(yy, s):
        total = lax.dot_general(slab(z1o, yy, s), go[...], TURNED, preferred_element_type=F32)
        total += lax.dot_general(slab(z1p, yy, s), gr[...], TURNED, preferred_element_type=F32)
        p2[yy, pl.ds(s * size, size)] = total.astype(BF16).reshape((size,) + p2.shape[2:])

    def pieces(s):
        return range(s * size, (s + 1) * size)

    def to_far(held, yy, s, far_in, far_sem, sides):
        for p in pieces(s):
            send(held.at[yy, p], far_in.at[p], far_sem.at[p], sides[p % 2])

    y_far, x_far = mod4(y + 2), home(mod4(x + 2))
    first_part(y_far, 0)
    to_far(p1, y_far, 0, ry2, sy2, y_sides)
    arrived(gr, gs.at[0])

    def all_of_z1p(step, carry):
        for zz in range(2):
            for chunk in range(CHUNKS):
                arrived(z1p.at[step, part(chunk), zz], k1s.at[step, zz, chunk])
        return carry

    lax.fori_loop(0, 4, all_of_z1p, 0)
    for s in range(2):
        second_part(x_far, s)
        to_far(p2, x_far, s, rx2, sx2, x_sides)
    first_part(y_far, 1)
    to_far(p1, y_far, 1, ry2, sy2, y_sides)

    def to_near(held, ahead, s, far_in, far_sem, near_in, near_sem, sides):
        for p in pieces(s):
            side = 1 - p % 2
            send(held.at[ahead[side], p], near_in.at[side, p], near_sem.at[side, p], sides[side])

    def to_near_with(held, ahead, s, far_in, far_sem, near_in, near_sem, sides):
        for p in pieces(s):
            side = p % 2
            arrived(far_in.at[p], far_sem.at[p])
            yy = ahead[side]
            held[yy, p] = (held[yy, p].astype(F32) + far_in[p].astype(F32)).astype(BF16)
            send(held.at[yy, p], near_in.at[side, p], near_sem.at[side, p], sides[side])

    for s in range(2):
        def near_x(step, carry):
            second_part(home(mod4(x + 1 + 2 * step)), s)
            return carry

        def near_y(step, carry):
            first_part(mod4(y + 1 + 2 * step), s)
            return carry

        along_x = (p2, (home(xr), home(xl)), s, rx2, sx2, rx1, sx1, x_sides)
        along_y = (p1, (yr, yl), s, ry2, sy2, ry1, sy1, y_sides)
        lax.fori_loop(0, 2, near_x, 0)
        to_near(*along_x)
        lax.fori_loop(0, 2, near_y, 0)
        to_near(*along_y)
        to_near_with(*along_x)
        to_near_with(*along_y)

    def own(step, carry):
        second_part(home(x), step)
        first_part(y, step)
        return carry

    lax.fori_loop(0, 2, own, 0)

    for p in range(PIECES + LAG):
        if p < PIECES:
            for side in range(2):
                arrived(rx1.at[side, p], sx1.at[side, p])
            value = p2[home(x), p].astype(F32) + rx1[0, p].astype(F32) + rx1[1, p].astype(F32)
            p2[home(x), p] = value.astype(BF16)
            for zz in range(2):
                stays = jnp.logical_and(zl == zh, zl == zz)
                send(
                    p2.at[home(x), p, zz], rz.at[zh, p], sz.at[zh, p], dev(zh=zl, zl=zz), jnp.logical_not(stays)
                )

                @pl.when(stays)
                def _():
                    rz[zh, p] = p2[home(x), p, zz]

            for side in range(2):
                arrived(ry1.at[side, p], sy1.at[side, p])

            def of_y(zz):
                return (
                    p1[y, p, zz].astype(F32) + ry1[0, p, zz].astype(F32) + ry1[1, p, zz].astype(F32)
                )

            p1[y, p, 1 - zl] = of_y(1 - zl).astype(BF16)
            send(p1.at[y, p, 1 - zl], rzl.at[p], szl.at[p], dev(zl=1 - zl))
        if p >= LAG:
            q = p - LAG
            for source in range(2):
                arrived(rz.at[source, q], sz.at[source, q], jnp.logical_or(crossed, zh != source))
            value = (rz[0, q].astype(F32) + rz[1, q].astype(F32)).astype(BF16)
            o2[q] = value
            fin_out[q] = value
            send(fin_out.at[q], fin_in.at[q], sfin.at[q], t_source, moved)
            arrived(rzl.at[q], szl.at[q])
            value = p1[y, q, zl].astype(F32) + ry1[0, q, zl].astype(F32) + ry1[1, q, zl].astype(F32)
            o1[q] = (value + rzl[q].astype(F32)).astype(BF16)

    for p in range(PIECES):
        arrived(fin_in.at[p], sfin.at[p], moved)

        @pl.when(moved)
        def _():
            o2[p] = fin_in[p]

    for copy, cond in started:
        if cond is None:
            copy.wait_send()
        else:
            pl.when(cond)(copy.wait_send)


SENDS = 320


def per_device(view_one, view_two, pair_weights):
    n = PIECES
    rows, depth = view_one.shape
    piece = (rows // n, depth)
    vmem = lambda *lead: pltpu.VMEM(lead + piece, BF16)
    square = (depth, depth)
    dma = lambda *shape: pltpu.SemaphoreType.DMA(shape)
    cut = (n,) + piece
    flops = 2 * 3 * 8 * rows * 2 * depth * depth
    first, second = pl.pallas_call(
        kernel,
        out_shape=[jax.ShapeDtypeStruct(cut, BF16)] * 2,
        in_specs=[
            pl.BlockSpec(memory_space=pltpu.HBM),
            pl.BlockSpec(memory_space=pltpu.HBM),
            pl.BlockSpec(memory_space=pltpu.VMEM),
        ],
        out_specs=[pl.BlockSpec(memory_space=pltpu.VMEM)] * 2,
        scratch_shapes=[
            vmem(4, n, 2), vmem(4, n, 2), vmem(5, n, 2), vmem(4, n, 2),
            pltpu.VMEM((2,) + square, F32),
            pltpu.VMEM(square, BF16), pltpu.VMEM(square, BF16), pltpu.VMEM(square, BF16),
            vmem(4, n, 2), vmem(4, n, 2),
            vmem(n, 2), vmem(2, n, 2), vmem(2, n),
            vmem(n, 2), vmem(2, n, 2), vmem(n), vmem(n), vmem(n),
            dma(1), dma(SENDS), dma(4, 2, CHUNKS), dma(4, 2, CHUNKS), dma(1), dma(2, 2), dma(2, 2, CHUNKS // 2),
            dma(CHUNKS), dma(2, CHUNKS), dma(2, 2, CHUNKS), dma(2, CHUNKS), dma(1),
            dma(n), dma(2, n), dma(2, n), dma(n), dma(2, n), dma(n), dma(n),
        ],
        compiler_params=pltpu.CompilerParams(
            collective_id=0, has_side_effects=True, vmem_limit_bytes=60 * 1024 * 1024
        ),
        cost_estimate=pl.CostEstimate(flops=flops, bytes_accessed=8 * rows * depth, transcendentals=0),
    )(view_one.reshape(cut), view_two.reshape(cut), pair_weights.reshape((2,) + square))
    return first.reshape(rows, depth), second.reshape(rows, depth)


def solution(mesh):
    placed = (P("row", "col"),) * 3
    return jax.shard_map(
        per_device, mesh=mesh, in_specs=placed, out_specs=(P("row", "col"),) * 2, check_vma=False
    )
```

time: 565 us -> 134 us (0.24)
  the two profiles are of different devices: /device:TPU:0 before, /device:TPU:35 now
where the time goes in v2:
time: 134 us
  Pallas kernels  131 us (98%)
  local copies, waits for them, and re-layouts  2.72 us (2%)
    pallas_call x1, Pallas kernels, per_device(): pl.pallas_call(kernel, out_shape=[jax.ShapeDtypeStruct(cut, BF16)] * 2, i...  131 us
    unnamed x4, local copies, waits for them, and re-layouts  2.72 us

profile of v2, /device:TPU:35, one launch (start us, length us, event | category | flops | bytes accessed | tf_op | source)
XLA Modules:
  0.0 134.0 jit_solution(15913111928380744915)
XLA Ops:
  0.6 130.6 %shard_map.50 = (bf16[8,64,512]{2,1,0:T(8,128)(2,1)}, bf16[8,64,512]{2,1,0:T(8,128)(2,1)}) custom-call(bf16[8,64,512]{2,1,0:T(8,128)(2,1)} %bitcast.8, bf16[8,64,512]{2,1,0:T(8,128)(2,1)} %bitcast.9, bf16[2,512,512]{2,1,0:T(8,128)(2,1)} %bitcast.7), custom_call_target="tpu_custom_call" | custom-call | flops 12884901888 | bytes 2097152 | tf_op jit(solution)/shard_map/pallas_call | solution.py:366
  131.2 0.0 copy-start
  131.3 1.9 %copy.7 = bf16[512,512]{1,0:T(8,128)(2,1)} copy(bf16[512,512]{1,0:T(8,128)(2,1)} %bitcast.6) | data formatting | bytes 1048576
  133.2 0.0 copy-done
  133.2 0.8 copy.8
Async XLA Ops:
  131.2 1.9 %copy-start = (bf16[8,64,512]{2,1,0:T(8,128)(2,1)S(1)}, bf16[8,64,512]{2,1,0:T(8,128)(2,1)}, u32[]{:S(2)}) copy-start(bf16[8,64,512]{2,1,0:T(8,128)(2,1)} %get-tuple-element.5) | copy-start | bytes 1572868

commit v3 on v2

v3 whole, which is shorter than its diff:
```python
import functools

import jax
import jax.numpy as jnp
from jax import lax
from jax.experimental import pallas as pl
from jax.experimental.pallas import tpu as pltpu
from jax.sharding import PartitionSpec as P

F32 = jnp.float32
BF16 = jnp.bfloat16
PIECES = 8
CHUNKS = 4
WIDE = PIECES // CHUNKS
LAG = 2
YLAG = 1
SEQUENCE = tuple(range(PIECES))
TURNED = (((1,), (1,)), ((), ()))


def kernel(
    v1, v2, w_hbm, o1, o2,
    w, z1o, z1p, z2o, z2p, acc, go, gp, gr, p1, p2, rx2, rx1, rz, ry2, ry1, rzl, fin_out, fin_in,
    lsem, ssem, k1s, k2s, zls, y1s, y2s, ts, rs, us, x1s, x2s, gs, sx2, sx1, sz, sy2, sy1, szl, sfin,
):
    row, col = lax.axis_index("row"), lax.axis_index("col")
    y, zl = row // 2, row % 2
    x, zh, k = col // 4, (col // 2) % 2, col % 2
    depth = v1.shape[2]
    samples = v1.shape[0] * v1.shape[1] * 8
    tile = min(256, depth)

    def dev(x=x, y=y, zh=zh, zl=zl, k=k):
        return (y * 2 + zl, x * 4 + zh * 2 + k)

    def mod4(a):
        return (a + 8) % 4

    xr, xl, yr, yl = mod4(x + 1), mod4(x - 1), mod4(y + 1), mod4(y - 1)
    d = mod4(x - y)
    moved = d != 0
    crossed = zh != zl
    straight = zh == zl
    partner = dev(k=1 - k)
    x_sides = (dev(x=xr), dev(x=xl))
    y_sides = (dev(y=yr), dev(y=yl))

    groups = []

    def send(src, dst, recv, where, cond=None):
        size = 1
        for extent in src.shape[:-2]:
            size *= extent
        if len(src.shape) == 2 and src.shape != v1.shape[1:]:
            size = GROUP
        for group in groups:
            if group[0] == size and group[1] is cond and group[2] + size <= GROUP:
                break
        else:
            group = [size, cond, 0, len(groups)]
            groups.append(group)
        group[2] += size
        copy = pltpu.make_async_remote_copy(
            src_ref=src, dst_ref=dst, send_sem=ssem.at[group[3]], recv_sem=recv,
            device_id=where, device_id_type=pl.DeviceIdType.MESH,
        )
        if cond is None:
            copy.start()
        else:
            pl.when(cond)(copy.start)

    def arrived(dst, recv, cond=None):
        copy = pltpu.make_async_remote_copy(
            src_ref=dst, dst_ref=dst, send_sem=ssem.at[0], recv_sem=recv,
            device_id=partner, device_id_type=pl.DeviceIdType.MESH,
        )
        if cond is None:
            copy.wait_recv()
        else:
            pl.when(cond)(copy.wait_recv)

    def home(xx, half):
        return mod4(2 * y - xx + (2 * (xx % 2) - 1) * half)

    t_dest = [dev(x=mod4(x + d + (1 - 2 * (y % 2)) * half), y=x) for half in range(2)]
    t_source = [dev(x=y, y=home(x, half)) for half in range(2)]

    def part(chunk):
        return pl.ds(chunk * WIDE, WIDE)

    load = pltpu.make_async_copy(v1, z1o.at[y, :, zl], lsem.at[0])
    load.start()
    fetch = pltpu.make_async_copy(w_hbm, w, lsem.at[1])
    fetch.start()
    barrier = pltpu.get_barrier_semaphore()
    for where in x_sides + y_sides + (
        partner, dev(zl=1 - zl), dev(zh=1 - zh), dev(zh=1 - zh, zl=1 - zl),
        t_dest[1], t_source[1],
    ):
        pl.semaphore_signal(barrier, inc=1, device_id=where, device_id_type=pl.DeviceIdType.MESH)

    @pl.when(moved)
    def _():
        pl.semaphore_signal(barrier, inc=1, device_id=t_dest[0], device_id_type=pl.DeviceIdType.MESH)
        pl.semaphore_signal(barrier, inc=1, device_id=t_source[0], device_id_type=pl.DeviceIdType.MESH)

    pl.semaphore_wait(barrier, jnp.where(moved, 12, 10))

    spare = jnp.where(crossed, 0, zl)

    def landing(yy, chunk):
        return z2o.at[jnp.where(crossed, 4, yy), part(chunk), spare]

    def local(chunk):
        return pltpu.make_async_copy(v2.at[part(chunk)], landing(home(x, 0), chunk), ts.at[chunk])

    order = (0, 2, 1, 3)
    for chunk in order:
        half = chunk // 2
        send(v2.at[part(chunk)], landing(y, chunk), ts.at[chunk], t_dest[half], None if half else moved)
        if half == 0:
            pl.when(d == 0)(local(chunk).start)

    def share1(yy, zz, chunk):
        block = z1o.at[yy, part(chunk), zz]
        send(block, z1p.at[yy, part(chunk), zz], k1s.at[0], partner)

    def share2(xx, zz, chunk, cond=None):
        block = held2(xx, zz, chunk)
        send(block, z2p.at[home(xx, chunk // 2), part(chunk), zz], k2s.at[home(xx, chunk // 2), chunk // 2], partner, cond)

    def held2(xx, zz, chunk):
        return z2o.at[home(xx, chunk // 2), part(chunk), zz]

    load.wait()

    def y_spread(number, zz, chunk):
        block = z1o.at[y, part(chunk), zz]
        for side in range(2):
            send(block, block, y1s.at[side, number, chunk], y_sides[side])

    def zl_swap(chunk):
        block = z1o.at[y, part(chunk), zl]
        send(block, block, zls.at[chunk], dev(zl=1 - zl))

    def x_spread(zz, chunk, cond):
        block = held2(x, zz, chunk)
        for side in range(2):
            send(block, block, x1s.at[side, zz, chunk], x_sides[side], cond)
        share2(x, zz, chunk, cond)

    def z_move(chunk):
        here = landing(home(x, chunk // 2), chunk)
        if chunk // 2:
            arrived(here, ts.at[chunk])
        else:
            arrived(here, ts.at[chunk], moved)
            pl.when(d == 0)(local(chunk).wait)
        there = held2(x, zl, chunk)
        for target in (dev(zh=1 - zl, zl=zh), dev(zh=zl, zl=zh)):
            send(here, there, us.at[zl, chunk], target, crossed)
        send(here, z2o.at[4, part(chunk), 0], rs.at[chunk], dev(zh=1 - zh, zl=1 - zl), straight)
        x_spread(zl, chunk, straight)

    def relay(chunk):
        here = z2o.at[4, part(chunk), 0]
        arrived(here, rs.at[chunk], straight)
        send(here, held2(x, 1 - zl, chunk), us.at[1 - zl, chunk], dev(zl=1 - zl), straight)

    def x_direct(chunk):
        arrived(held2(x, 1 - zl, chunk), us.at[1 - zl, chunk])
        x_spread(1 - zl, chunk, None)

    def x_relayed(chunk):
        arrived(held2(x, zl, chunk), us.at[zl, chunk], crossed)
        x_spread(zl, chunk, crossed)

    def y_forward(number, chunk):
        zz = zl if number == 0 else 1 - zl
        for side, source in enumerate((yl, yr)):
            block = z1o.at[source, part(chunk), zz]
            arrived(block, y1s.at[side, number, chunk])
            if chunk % 2 == side:
                send(block, block, y2s.at[number, chunk], y_sides[side])
            share1(source, zz, chunk)

    def x_forward(chunk):
        for zz in range(2):
            for side, source in enumerate((xl, xr)):
                block = held2(source, zz, chunk)
                arrived(block, x1s.at[side, zz, chunk])
                if chunk % 2 == side:
                    send(block, block, x2s.at[zz, chunk], x_sides[side])
                share2(source, zz, chunk)

    def zl_step(chunk):
        arrived(z1o.at[y, part(chunk), 1 - zl], zls.at[chunk])
        y_spread(1, 1 - zl, chunk)
        share1(y, 1 - zl, chunk)

    a, b, c, e = order
    zl_swap(a)
    for chunk in order:
        y_spread(0, zl, chunk)
    for chunk in order:
        z_move(chunk)
    zl_swap(b)
    zl_step(a)
    for chunk in order:
        share1(y, zl, chunk)
    x_direct(a)
    relay(a)
    x_direct(b)
    relay(b)
    zl_swap(c)
    x_direct(c)
    relay(c)
    x_relayed(a)
    zl_swap(e)
    x_direct(e)
    relay(e)
    x_relayed(b)
    y_forward(0, a)
    y_forward(0, b)
    zl_step(b)
    x_relayed(c)
    y_forward(0, c)
    y_forward(0, e)
    zl_step(c)
    x_relayed(e)
    x_forward(a)
    zl_step(e)
    y_forward(1, a)
    x_forward(b)
    y_forward(1, b)
    x_forward(c)
    y_forward(1, c)
    x_forward(e)
    y_forward(1, e)

    size = PIECES // 2

    def slab(ref, yy, s, columns=slice(None)):
        block = ref[yy, pl.ds(s * size, size), :, :, columns]
        return block.reshape(-1, block.shape[-1])

    def correlate(yy, s):
        arrived(z2p.at[yy, pl.ds(s * size, size)], k2s.at[yy, s])
        right = slab(z1o, yy, s)
        for number, held in enumerate((z2o, z2p)):
            for start in range(0, depth, tile):
                left = slab(held, yy, s, pl.ds(start, tile))
                acc[number, pl.ds(start, tile), :] += lax.dot_general(
                    left, right, (((0,), (0,)), ((), ())), preferred_element_type=F32
                )

    def last_along_y(half):
        return mod4(2 - d + (1 - 2 * (y % 2)) * half)

    def early(step, carry):
        half = step % 2
        late_one = last_along_y(half)
        first = jnp.where(late_one == 0, 1, 0)
        second = jnp.where(late_one < 2, 3, 1)
        correlate(home(mod4(x + jnp.where(step < 2, first, second)), half), half)
        return carry

    acc[...] = jnp.zeros_like(acc)
    lax.fori_loop(0, 4, early, 0)
    for number in range(2):
        zz = zl if number == 0 else 1 - zl
        for chunk in range(CHUNKS):
            arrived(z1o.at[mod4(y + 2), part(chunk), zz], y2s.at[number, chunk])
            share1(mod4(y + 2), zz, chunk)

    def third(step, carry):
        late_one = last_along_y(step)
        correlate(home(mod4(x + jnp.where(late_one == 2, 3, late_one)), step), step)
        return carry

    lax.fori_loop(0, 2, third, 0)
    for chunk in order:
        for zz in range(2):
            arrived(held2(mod4(x + 2), zz, chunk), x2s.at[zz, chunk])
            share2(mod4(x + 2), zz, chunk)

    def last(step, carry):
        correlate(home(mod4(x + 2), step), step)
        return carry

    lax.fori_loop(0, 2, last, 0)

    def weigh(number, target):
        half = k if number == 0 else 1 - k
        for start in range(0, depth, tile):
            shape = (tile, depth)
            row_ids = row * (2 * depth) + half * depth + start + lax.broadcasted_iota(jnp.int32, shape, 0)
            col_ids = col * depth + lax.broadcasted_iota(jnp.int32, shape, 1)
            identity = jnp.where(row_ids == col_ids, 1.0, 0.0).astype(F32)
            correlation = acc[number, pl.ds(start, tile), :] / samples
            weights = w[half, pl.ds(start, tile), :].astype(F32)
            target[pl.ds(start, tile), :] = (weights * (correlation - identity)).astype(BF16)

    fetch.wait()
    weigh(1, gp)
    send(gp, gr, gs.at[0], partner)
    weigh(0, go)
    arrived(z1p, k1s.at[0])

    def first_part(yy, s):
        total = jnp.dot(slab(z2o, yy, s), go[...], preferred_element_type=F32)
        total += jnp.dot(slab(z2p, yy, s), gp[...], preferred_element_type=F32)
        p1[yy, pl.ds(s * size, size)] = total.astype(BF16).reshape((size,) + p1.shape[2:])

    def second_part(yy, s, ready=None):
        total = lax.dot_general(slab(z1o, yy, s), go[...], TURNED, preferred_element_type=F32)
        if ready is not None:
            ready()
        total += lax.dot_general(slab(z1p, yy, s), gr[...], TURNED, preferred_element_type=F32)
        p2[yy, pl.ds(s * size, size)] = total.astype(BF16).reshape((size,) + p2.shape[2:])

    def pieces(s):
        return range(s * size, (s + 1) * size)

    def to_far(held, yy, s, far_in, far_sem, sides):
        for p in pieces(s):
            send(held.at[yy, p], far_in.at[p], far_sem.at[p], sides[p % 2])

    def far_x(s, ready=None):
        second_part(home(mod4(x + 2), s), s, ready)
        to_far(p2, home(mod4(x + 2), s), s, rx2, sx2, x_sides)

    def far_y(s):
        first_part(mod4(y + 2), s)
        to_far(p1, mod4(y + 2), s, ry2, sy2, y_sides)

    far_y(0)
    far_x(0, lambda: arrived(gr, gs.at[0]))
    far_x(1)
    far_y(1)

    def to_near(held, ahead, p, far_in, far_sem, near_in, near_sem, sides, which=(0, 1)):
        for side in which:
            yy = ahead[side]
            if p % 2 == side:
                arrived(far_in.at[p], far_sem.at[p])
                held[yy, p] = (held[yy, p].astype(F32) + far_in[p].astype(F32)).astype(BF16)
            send(held.at[yy, p], near_in.at[side, p], near_sem.at[side, p], sides[side])

    def along_x(p, which=(0, 1)):
        to_near(p2, (home(xr, p // size), home(xl, p // size)), p, rx2, sx2, rx1, sx1, x_sides, which)

    def along_y(p, which=(0, 1)):
        to_near(p1, (yr, yl), p, ry2, sy2, ry1, sy1, y_sides, which)

    for s in range(2):
        def near_x(step, carry):
            second_part(home(mod4(x + 1 + 2 * step), s), s)
            return carry

        def near_y(step, carry):
            first_part(mod4(y + 1 + 2 * step), s)
            return carry

        lax.fori_loop(0, 2, near_x, 0)
        for p in range(s * size, (s + 1) * size):
            along_x(p)
        lax.fori_loop(0, 2, near_y, 0)
        for p in range(s * size, (s + 1) * size):
            along_y(p)

    def own(step, carry):
        second_part(home(x, step), step)
        first_part(y, step)
        return carry

    lax.fori_loop(0, 2, own, 0)

    goes = [jnp.logical_or(crossed, zl != zz) for zz in range(2)]

    def x_total(p):
        here = home(x, p // size)
        for side in range(2):
            arrived(rx1.at[side, p], sx1.at[side, p])
        value = p2[here, p].astype(F32) + rx1[0, p].astype(F32) + rx1[1, p].astype(F32)
        p2[here, p] = value.astype(BF16)
        for zz in range(2):
            send(p2.at[here, p, zz], rz.at[zh, p], sz.at[zh, p], dev(zh=zl, zl=zz), goes[zz])

            @pl.when(jnp.logical_not(goes[zz]))
            def _():
                rz[zh, p] = p2[here, p, zz]

    def x_final(p):
        for source in range(2):
            arrived(rz.at[source, p], sz.at[source, p], jnp.logical_or(crossed, zh != source))
        value = (rz[0, p].astype(F32) + rz[1, p].astype(F32)).astype(BF16)
        fin_out[p] = value
        if p < size:
            o2[p] = value
            send(fin_out.at[p], fin_in.at[p], sfin.at[p], t_source[0], moved)
        else:
            send(fin_out.at[p], fin_in.at[p], sfin.at[p], t_source[1])

    def of_y(p, zz):
        return p1[y, p, zz].astype(F32) + ry1[0, p, zz].astype(F32) + ry1[1, p, zz].astype(F32)

    def y_total(p):
        for side in range(2):
            arrived(ry1.at[side, p], sy1.at[side, p])
        p1[y, p, 1 - zl] = of_y(p, 1 - zl).astype(BF16)
        send(p1.at[y, p, 1 - zl], rzl.at[p], szl.at[p], dev(zl=1 - zl))

    def y_final(p):
        arrived(rzl.at[p], szl.at[p])
        o1[p] = (of_y(p, zl) + rzl[p].astype(F32)).astype(BF16)

    for turn in range(PIECES + LAG + YLAG):
        for lag, stage in ((0, x_total), (LAG, x_final), (YLAG, y_total), (LAG + YLAG, y_final)):
            if 0 <= turn - lag < PIECES:
                stage(SEQUENCE[turn - lag])

    for p in SEQUENCE:
        if p < size:
            arrived(fin_in.at[p], sfin.at[p], moved)

            @pl.when(moved)
            def _():
                o2[p] = fin_in[p]
        else:
            arrived(fin_in.at[p], sfin.at[p])
            o2[p] = fin_in[p]

    for size, cond, pieces_sent, number in groups:
        if size == GROUP:
            ref = gp
        elif pieces_sent % 2:
            ref = z1p.at[0, pl.ds(0, pieces_sent), 0]
        else:
            ref = z1p.at[0, pl.ds(0, pieces_sent // 2)]
        copy = pltpu.make_async_remote_copy(
            src_ref=ref, dst_ref=ref, send_sem=ssem.at[number], recv_sem=ssem.at[number],
            device_id=partner, device_id_type=pl.DeviceIdType.MESH,
        )
        if cond is None:
            copy.wait_send()
        else:
            pl.when(cond)(copy.wait_send)


GROUP = 2 * PIECES
SENDS = 56


def per_device(view_one, view_two, pair_weights):
    n = PIECES
    rows, depth = view_one.shape
    piece = (rows // n, depth)
    vmem = lambda *lead: pltpu.VMEM(lead + piece, BF16)
    square = (depth, depth)
    dma = lambda *shape: pltpu.SemaphoreType.DMA(shape)
    cut = (n,) + piece
    flops = 2 * 3 * 8 * rows * 2 * depth * depth
    first, second = pl.pallas_call(
        kernel,
        out_shape=[jax.ShapeDtypeStruct(cut, BF16)] * 2,
        in_specs=[
            pl.BlockSpec(memory_space=pltpu.HBM),
            pl.BlockSpec(memory_space=pltpu.HBM),
            pl.BlockSpec(memory_space=pltpu.HBM),
        ],
        out_specs=[pl.BlockSpec(memory_space=pltpu.VMEM)] * 2,
        scratch_shapes=[
            pltpu.VMEM((2,) + square, BF16),
            vmem(4, n, 2), vmem(4, n, 2), vmem(5, n, 2), vmem(4, n, 2),
            pltpu.VMEM((2,) + square, F32),
            pltpu.VMEM(square, BF16), pltpu.VMEM(square, BF16), pltpu.VMEM(square, BF16),
            vmem(4, n, 2), vmem(4, n, 2),
            vmem(n, 2), vmem(2, n, 2), vmem(2, n),
            vmem(n, 2), vmem(2, n, 2), vmem(n), vmem(n), vmem(n),
            dma(2), dma(SENDS), dma(1), dma(4, 2), dma(CHUNKS), dma(2, 2, CHUNKS), dma(2, CHUNKS),
            dma(CHUNKS), dma(CHUNKS), dma(2, CHUNKS), dma(2, 2, CHUNKS), dma(2, CHUNKS), dma(1),
            dma(n), dma(2, n), dma(2, n), dma(n), dma(2, n), dma(n), dma(n),
        ],
        compiler_params=pltpu.CompilerParams(
            collective_id=0, has_side_effects=True, vmem_limit_bytes=60 * 1024 * 1024
        ),
        cost_estimate=pl.CostEstimate(flops=flops, bytes_accessed=8 * rows * depth, transcendentals=0),
    )(view_one.reshape(cut), view_two.reshape(cut), pair_weights.reshape((2,) + square))
    return first.reshape(rows, depth), second.reshape(rows, depth)


def solution(mesh):
    placed = (P("row", "col"),) * 3
    return jax.shard_map(
        per_device, mesh=mesh, in_specs=placed, out_specs=(P("row", "col"),) * 2, check_vma=False
    )
```

time: 134 us -> 122 us (0.910)
  the two profiles are of different devices: /device:TPU:35 before, /device:TPU:48 now
where the time goes in v3:
time: 122 us
  Pallas kernels  118 us (97%)
  local copies, waits for them, and re-layouts  2.72 us (2%)
    pallas_call x1, Pallas kernels, per_device(): pl.pallas_call(kernel, out_shape=[jax.ShapeDtypeStruct(cut, BF16)] * 2, i...  118 us
    unnamed x4, local copies, waits for them, and re-layouts  2.72 us

profile of v3, /device:TPU:48, one launch (start us, length us, event | category | flops | bytes accessed | tf_op | source)
XLA Modules:
  0.0 121.5 jit_solution(16516265007626871666)
XLA Ops:
  0.6 118.2 %shard_map.50 = (bf16[8,64,512]{2,1,0:T(8,128)(2,1)}, bf16[8,64,512]{2,1,0:T(8,128)(2,1)}) custom-call(bf16[8,64,512]{2,1,0:T(8,128)(2,1)} %bitcast.8, bf16[8,64,512]{2,1,0:T(8,128)(2,1)} %bitcast.9, bf16[2,512,512]{2,1,0:T(8,128)(2,1)} %bitcast.7), custom_call_target="tpu_custom_call" | custom-call | flops 12884901888 | bytes 2097152 | tf_op jit(solution)/shard_map/pallas_call | solution.py:464
  118.8 0.0 copy-start
  118.8 1.9 %copy.7 = bf16[512,512]{1,0:T(8,128)(2,1)} copy(bf16[512,512]{1,0:T(8,128)(2,1)} %bitcast.6) | data formatting | bytes 1048576
  120.7 0.0 copy-done
  120.7 0.8 copy.8
Async XLA Ops:
  118.8 1.9 %copy-start = (bf16[8,64,512]{2,1,0:T(8,128)(2,1)S(1)}, bf16[8,64,512]{2,1,0:T(8,128)(2,1)}, u32[]{:S(2)}) copy-start(bf16[8,64,512]{2,1,0:T(8,128)(2,1)} %get-tuple-element.5) | copy-start | bytes 1572868

commit v4 on v3

--- a/solution.py
+++ b/solution.py
@@ -13,15 +13,16 @@
 CHUNKS = 4
 WIDE = PIECES // CHUNKS
 LAG = 2
-YLAG = 1
-SEQUENCE = tuple(range(PIECES))
+AHEAD = 3
+ONWARD = 5
+Y_LAG = 4
 TURNED = (((1,), (1,)), ((), ()))
 
 
 def kernel(
     v1, v2, w_hbm, o1, o2,
-    w, z1o, z1p, z2o, z2p, acc, go, gp, gr, p1, p2, rx2, rx1, rz, ry2, ry1, rzl, fin_out, fin_in,
-    lsem, ssem, k1s, k2s, zls, y1s, y2s, ts, rs, us, x1s, x2s, gs, sx2, sx1, sz, sy2, sy1, szl, sfin,
+    w, z1o, z1p, z2o, z2p, acc, go, gp, gr, p1, p2, rx2, rx1, rz, ry2, ry1, rzl, fin_out, mid, fin_in, tally,
+    lsem, ssem, k1s, k2s, zls, y1s, y2s, ts, rs, us, x1s, x2s, gs, sx2, sx1, sz, sy2, sy1, szl, smid, sfin,
 ):
     row, col = lax.axis_index("row"), lax.axis_index("col")
     y, zl = row // 2, row % 2
@@ -37,8 +38,6 @@
         return (a + 8) % 4
 
     xr, xl, yr, yl = mod4(x + 1), mod4(x - 1), mod4(y + 1), mod4(y - 1)
-    d = mod4(x - y)
-    moved = d != 0
     crossed = zh != zl
     straight = zh == zl
     partner = dev(k=1 - k)
@@ -80,10 +79,13 @@
             pl.when(cond)(copy.wait_recv)
 
     def home(xx, half):
-        return mod4(2 * y - xx + (2 * (xx % 2) - 1) * half)
-
-    t_dest = [dev(x=mod4(x + d + (1 - 2 * (y % 2)) * half), y=x) for half in range(2)]
+        return mod4(y - xx + 2 * half)
+
+    t_dest = [dev(x=mod4(x - y + 2 * half), y=x) for half in range(2)]
     t_source = [dev(x=y, y=home(x, half)) for half in range(2)]
+    moves_y = [x != 2 * half for half in range(2)]
+    moves_x = [y != 2 * half for half in range(2)]
+    moved = [jnp.logical_or(moves_x[half], moves_y[half]) for half in range(2)]
 
     def part(chunk):
         return pl.ds(chunk * WIDE, WIDE)
@@ -94,17 +96,17 @@
     fetch.start()
     barrier = pltpu.get_barrier_semaphore()
     for where in x_sides + y_sides + (
-        partner, dev(zl=1 - zl), dev(zh=1 - zh), dev(zh=1 - zh, zl=1 - zl),
-        t_dest[1], t_source[1],
+        partner, dev(zl=1 - zl), dev(zh=1 - zh), dev(zh=1 - zh, zl=1 - zl), dev(x=mod4(x + 2)), dev(y=mod4(y + 2)),
     ):
         pl.semaphore_signal(barrier, inc=1, device_id=where, device_id_type=pl.DeviceIdType.MESH)
-
-    @pl.when(moved)
-    def _():
-        pl.semaphore_signal(barrier, inc=1, device_id=t_dest[0], device_id_type=pl.DeviceIdType.MESH)
-        pl.semaphore_signal(barrier, inc=1, device_id=t_source[0], device_id_type=pl.DeviceIdType.MESH)
-
-    pl.semaphore_wait(barrier, jnp.where(moved, 12, 10))
+    for half in range(2):
+        @pl.when(moved[half])
+        def _():
+            for where in (t_dest[half], t_source[half]):
+                pl.semaphore_signal(barrier, inc=1, device_id=where, device_id_type=pl.DeviceIdType.MESH)
+
+    own_blocks = jnp.logical_and(x == y, x % 2 == 0)
+    pl.semaphore_wait(barrier, jnp.where(own_blocks, 12, 14))
 
     spare = jnp.where(crossed, 0, zl)
 
@@ -112,14 +114,13 @@
         return z2o.at[jnp.where(crossed, 4, yy), part(chunk), spare]
 
     def local(chunk):
-        return pltpu.make_async_copy(v2.at[part(chunk)], landing(home(x, 0), chunk), ts.at[chunk])
+        return pltpu.make_async_copy(v2.at[part(chunk)], landing(home(x, chunk // 2), chunk), ts.at[chunk])
 
     order = (0, 2, 1, 3)
     for chunk in order:
         half = chunk // 2
-        send(v2.at[part(chunk)], landing(y, chunk), ts.at[chunk], t_dest[half], None if half else moved)
-        if half == 0:
-            pl.when(d == 0)(local(chunk).start)
+        send(v2.at[part(chunk)], landing(y, chunk), ts.at[chunk], t_dest[half], moved[half])
+        pl.when(jnp.logical_not(moved[half]))(local(chunk).start)
 
     def share1(yy, zz, chunk):
         block = z1o.at[yy, part(chunk), zz]
@@ -151,11 +152,8 @@
 
     def z_move(chunk):
         here = landing(home(x, chunk // 2), chunk)
-        if chunk // 2:
-            arrived(here, ts.at[chunk])
-        else:
-            arrived(here, ts.at[chunk], moved)
-            pl.when(d == 0)(local(chunk).wait)
+        arrived(here, ts.at[chunk], moved[chunk // 2])
+        pl.when(jnp.logical_not(moved[chunk // 2]))(local(chunk).wait)
         there = held2(x, zl, chunk)
         for target in (dev(zh=1 - zl, zl=zh), dev(zh=zl, zl=zh)):
             send(here, there, us.at[zl, chunk], target, crossed)
@@ -244,18 +242,27 @@
         block = ref[yy, pl.ds(s * size, size), :, :, columns]
         return block.reshape(-1, block.shape[-1])
 
+    def accumulate(number, held, yy, s):
+        right = slab(z1o, yy, s)
+        for start in range(0, depth, tile):
+            left = slab(held, yy, s, pl.ds(start, tile))
+            acc[number, pl.ds(start, tile), :] += lax.dot_general(
+                left, right, (((0,), (0,)), ((), ())), preferred_element_type=F32
+            )
+
+    def correlate_own(yy, s):
+        accumulate(0, z2o, yy, s)
+
+    def correlate_other(yy, s):
+        arrived(z2p.at[yy, pl.ds(s * size, size)], k2s.at[yy, s])
+        accumulate(1, z2p, yy, s)
+
     def correlate(yy, s):
-        arrived(z2p.at[yy, pl.ds(s * size, size)], k2s.at[yy, s])
-        right = slab(z1o, yy, s)
-        for number, held in enumerate((z2o, z2p)):
-            for start in range(0, depth, tile):
-                left = slab(held, yy, s, pl.ds(start, tile))
-                acc[number, pl.ds(start, tile), :] += lax.dot_general(
-                    left, right, (((0,), (0,)), ((), ())), preferred_element_type=F32
-                )
+        correlate_own(yy, s)
+        correlate_other(yy, s)
 
     def last_along_y(half):
-        return mod4(2 - d + (1 - 2 * (y % 2)) * half)
+        return mod4(2 - x + 2 * half)
 
     def early(step, carry):
         half = step % 2
@@ -284,11 +291,12 @@
             arrived(held2(mod4(x + 2), zz, chunk), x2s.at[zz, chunk])
             share2(mod4(x + 2), zz, chunk)
 
-    def last(step, carry):
-        correlate(home(mod4(x + 2), step), step)
-        return carry
-
-    lax.fori_loop(0, 2, last, 0)
+    for part_of in (correlate_own, correlate_other):
+        def last(step, carry):
+            part_of(home(mod4(x + 2), step), step)
+            return carry
+
+        lax.fori_loop(0, 2, last, 0)
 
     def weigh(number, target):
         half = k if number == 0 else 1 - k
@@ -334,8 +342,8 @@
         first_part(mod4(y + 2), s)
         to_far(p1, mod4(y + 2), s, ry2, sy2, y_sides)
 
+    far_x(0, lambda: arrived(gr, gs.at[0]))
     far_y(0)
-    far_x(0, lambda: arrived(gr, gs.at[0]))
     far_x(1)
     far_y(1)
 
@@ -363,11 +371,13 @@
             return carry
 
         lax.fori_loop(0, 2, near_x, 0)
-        for p in range(s * size, (s + 1) * size):
-            along_x(p)
+        if s == 0:
+            for p in range(size):
+                along_x(p)
         lax.fori_loop(0, 2, near_y, 0)
-        for p in range(s * size, (s + 1) * size):
-            along_y(p)
+        if s == 0:
+            for p in range(size):
+                along_y(p)
 
     def own(step, carry):
         second_part(home(x, step), step)
@@ -395,12 +405,22 @@
         for source in range(2):
             arrived(rz.at[source, p], sz.at[source, p], jnp.logical_or(crossed, zh != source))
         value = (rz[0, p].astype(F32) + rz[1, p].astype(F32)).astype(BF16)
+        half = p // size
         fin_out[p] = value
-        if p < size:
-            o2[p] = value
-            send(fin_out.at[p], fin_in.at[p], sfin.at[p], t_source[0], moved)
-        else:
-            send(fin_out.at[p], fin_in.at[p], sfin.at[p], t_source[1])
+        send(fin_out.at[p], mid.at[p], smid.at[p], dev(y=home(x, half)), moves_y[half])
+
+        @pl.when(jnp.logical_not(moves_y[half]))
+        def _():
+            mid[p] = value
+
+    def x_onward(p):
+        half = p // size
+        arrived(mid.at[p], smid.at[p], moves_y[half])
+        send(mid.at[p], fin_in.at[p], sfin.at[p], dev(x=mod4(x + y - 2 * half)), moves_x[half])
+
+        @pl.when(jnp.logical_not(moves_x[half]))
+        def _():
+            o2[p] = mid[p]
 
     def of_y(p, zz):
         return p1[y, p, zz].astype(F32) + ry1[0, p, zz].astype(F32) + ry1[1, p, zz].astype(F32)
@@ -415,29 +435,25 @@
         arrived(rzl.at[p], szl.at[p])
         o1[p] = (of_y(p, zl) + rzl[p].astype(F32)).astype(BF16)
 
-    for turn in range(PIECES + LAG + YLAG):
-        for lag, stage in ((0, x_total), (LAG, x_final), (YLAG, y_total), (LAG + YLAG, y_final)):
-            if 0 <= turn - lag < PIECES:
-                stage(SEQUENCE[turn - lag])
-
-    for p in SEQUENCE:
-        if p < size:
-            arrived(fin_in.at[p], sfin.at[p], moved)
-
-            @pl.when(moved)
-            def _():
-                o2[p] = fin_in[p]
-        else:
-            arrived(fin_in.at[p], sfin.at[p])
+    stages = (
+        (0, x_total), (-AHEAD, along_x), (LAG, x_final), (-AHEAD, along_y), (1, y_total), (ONWARD, x_onward),
+        (Y_LAG, y_final),
+    )
+    for turn in range(PIECES + max(ONWARD, Y_LAG)):
+        for lag, stage in stages:
+            if (size if lag < 0 else 0) <= turn - lag < PIECES:
+                stage(turn - lag)
+
+    for p in range(PIECES):
+        half = p // size
+        arrived(fin_in.at[p], sfin.at[p], moves_x[half])
+
+        @pl.when(moves_x[half])
+        def _():
             o2[p] = fin_in[p]
 
     for size, cond, pieces_sent, number in groups:
-        if size == GROUP:
-            ref = gp
-        elif pieces_sent % 2:
-            ref = z1p.at[0, pl.ds(0, pieces_sent), 0]
-        else:
-            ref = z1p.at[0, pl.ds(0, pieces_sent // 2)]
+        ref = gp if size == GROUP else tally.at[pl.ds(0, pieces_sent)]
         copy = pltpu.make_async_remote_copy(
             src_ref=ref, dst_ref=ref, send_sem=ssem.at[number], recv_sem=ssem.at[number],
             device_id=partner, device_id_type=pl.DeviceIdType.MESH,
@@ -448,8 +464,8 @@
             pl.when(cond)(copy.wait_send)
 
 
-GROUP = 2 * PIECES
-SENDS = 56
+GROUP = 8 * PIECES
+SENDS = 17
 
 
 def per_device(view_one, view_two, pair_weights):
@@ -477,13 +493,13 @@
             pltpu.VMEM(square, BF16), pltpu.VMEM(square, BF16), pltpu.VMEM(square, BF16),
             vmem(4, n, 2), vmem(4, n, 2),
             vmem(n, 2), vmem(2, n, 2), vmem(2, n),
-            vmem(n, 2), vmem(2, n, 2), vmem(n), vmem(n), vmem(n),
+            vmem(n, 2), vmem(2, n, 2), vmem(n), vmem(n), vmem(n), vmem(n), vmem(GROUP),
             dma(2), dma(SENDS), dma(1), dma(4, 2), dma(CHUNKS), dma(2, 2, CHUNKS), dma(2, CHUNKS),
             dma(CHUNKS), dma(CHUNKS), dma(2, CHUNKS), dma(2, 2, CHUNKS), dma(2, CHUNKS), dma(1),
-            dma(n), dma(2, n), dma(2, n), dma(n), dma(2, n), dma(n), dma(n),
+            dma(n), dma(2, n), dma(2, n), dma(n), dma(2, n), dma(n), dma(n), dma(n),
         ],
         compiler_params=pltpu.CompilerParams(
-            collective_id=0, has_side_effects=True, vmem_limit_bytes=60 * 1024 * 1024
+            collective_id=0, has_side_effects=True, vmem_limit_bytes=53 * 1024 * 1024
         ),
         cost_estimate=pl.CostEstimate(flops=flops, bytes_accessed=8 * rows * depth, transcendentals=0),
     )(view_one.reshape(cut), view_two.reshape(cut), pair_weights.reshape((2,) + square))

time: 122 us -> 112 us (0.918)
  the two profiles are of different devices: /device:TPU:48 before, /device:TPU:0 now
where the time goes in v4:
time: 112 us
  Pallas kernels  109 us (97%)
  local copies, waits for them, and re-layouts  2.02 us (2%)
    pallas_call x1, Pallas kernels, per_device(): pl.pallas_call(kernel, out_shape=[jax.ShapeDtypeStruct(cut, BF16)] * 2, i...  109 us

profile of v4, /device:TPU:0, one launch (start us, length us, event | category | flops | bytes accessed | tf_op | source)
XLA Modules:
  0.0 111.6 jit_solution(7810978999691040407)
XLA Ops:
  0.6 109.0 %shard_map.50 = (bf16[8,64,512]{2,1,0:T(8,128)(2,1)S(1)}, bf16[8,64,512]{2,1,0:T(8,128)(2,1)}) custom-call(bf16[8,64,512]{2,1,0:T(8,128)(2,1)} %bitcast.8, bf16[8,64,512]{2,1,0:T(8,128)(2,1)} %bitcast.9, bf16[2,512,512]{2,1,0:T(8,128)(2,1)} %bitcast.7), custom_call_target="tpu_custom_call" | custom-call | flops 12884901888 | bytes 2097152 | tf_op jit(solution)/shard_map/pallas_call | solution.py:480
  109.6 0.0 copy-start
  109.6 0.8 copy.7
  110.4 0.4 copy-done
  110.8 0.8 copy.8
Async XLA Ops:
  109.6 1.2 %copy-start = (bf16[8,64,512]{2,1,0:T(8,128)(2,1)S(1)}, bf16[8,64,512]{2,1,0:T(8,128)(2,1)}, u32[]{:S(2)}) copy-start(bf16[8,64,512]{2,1,0:T(8,128)(2,1)} %get-tuple-element.5) | copy-start | bytes 1572868

commit v5 on v4

--- a/solution.py
+++ b/solution.py
@@ -21,7 +21,7 @@
 
 def kernel(
     v1, v2, w_hbm, o1, o2,
-    w, z1o, z1p, z2o, z2p, acc, go, gp, gr, p1, p2, rx2, rx1, rz, ry2, ry1, rzl, fin_out, mid, fin_in, tally,
+    w, z1o, z1p, z2o, z2p, acc, go, gp, gr, p1, p2, rx2, rx1, rz, ry2, ry1, rzl, fin_out, mid, fin_in, tally, staged,
     lsem, ssem, k1s, k2s, zls, y1s, y2s, ts, rs, us, x1s, x2s, gs, sx2, sx1, sz, sy2, sy1, szl, smid, sfin,
 ):
     row, col = lax.axis_index("row"), lax.axis_index("col")
@@ -92,6 +92,8 @@
 
     load = pltpu.make_async_copy(v1, z1o.at[y, :, zl], lsem.at[0])
     load.start()
+    ready = pltpu.make_async_copy(v2, staged, lsem.at[2])
+    ready.start()
     fetch = pltpu.make_async_copy(w_hbm, w, lsem.at[1])
     fetch.start()
     barrier = pltpu.get_barrier_semaphore()
@@ -117,9 +119,10 @@
         return pltpu.make_async_copy(v2.at[part(chunk)], landing(home(x, chunk // 2), chunk), ts.at[chunk])
 
     order = (0, 2, 1, 3)
+    ready.wait()
     for chunk in order:
         half = chunk // 2
-        send(v2.at[part(chunk)], landing(y, chunk), ts.at[chunk], t_dest[half], moved[half])
+        send(staged.at[part(chunk)], landing(y, chunk), ts.at[chunk], t_dest[half], moved[half])
         pl.when(jnp.logical_not(moved[half]))(local(chunk).start)
 
     def share1(yy, zz, chunk):
@@ -493,8 +496,8 @@
             pltpu.VMEM(square, BF16), pltpu.VMEM(square, BF16), pltpu.VMEM(square, BF16),
             vmem(4, n, 2), vmem(4, n, 2),
             vmem(n, 2), vmem(2, n, 2), vmem(2, n),
-            vmem(n, 2), vmem(2, n, 2), vmem(n), vmem(n), vmem(n), vmem(n), vmem(GROUP),
-            dma(2), dma(SENDS), dma(1), dma(4, 2), dma(CHUNKS), dma(2, 2, CHUNKS), dma(2, CHUNKS),
+            vmem(n, 2), vmem(2, n, 2), vmem(n), vmem(n), vmem(n), vmem(n), vmem(GROUP), vmem(n),
+            dma(3), dma(SENDS), dma(1), dma(4, 2), dma(CHUNKS), dma(2, 2, CHUNKS), dma(2, CHUNKS),
             dma(CHUNKS), dma(CHUNKS), dma(2, CHUNKS), dma(2, 2, CHUNKS), dma(2, CHUNKS), dma(1),
             dma(n), dma(2, n), dma(2, n), dma(n), dma(2, n), dma(n), dma(n), dma(n),
         ],

time: 112 us -> 112 us (level)
  no operation moved by 1% of the time
where the time goes in v5:
time: 112 us
  Pallas kernels  109 us (97%)
  local copies, waits for them, and re-layouts  2.02 us (2%)
    pallas_call x1, Pallas kernels, per_device(): pl.pallas_call(kernel, out_shape=[jax.ShapeDtypeStruct(cut, BF16)] * 2, i...  109 us

profile of v5, /device:TPU:0, one launch (start us, length us, event | category | flops | bytes accessed | tf_op | source)
XLA Modules:
  0.0 111.6 jit_solution(10706640309411317128)
XLA Ops:
  0.6 109.0 %shard_map.50 = (bf16[8,64,512]{2,1,0:T(8,128)(2,1)S(1)}, bf16[8,64,512]{2,1,0:T(8,128)(2,1)}) custom-call(bf16[8,64,512]{2,1,0:T(8,128)(2,1)} %bitcast.8, bf16[8,64,512]{2,1,0:T(8,128)(2,1)} %bitcast.9, bf16[2,512,512]{2,1,0:T(8,128)(2,1)} %bitcast.7), custom_call_target="tpu_custom_call" | custom-call | flops 12884901888 | bytes 2097152 | tf_op jit(solution)/shard_map/pallas_call | solution.py:483
  109.6 0.0 copy-start
  109.6 0.8 copy.7
  110.4 0.4 copy-done
  110.8 0.8 copy.8
Async XLA Ops:
  109.6 1.2 %copy-start = (bf16[8,64,512]{2,1,0:T(8,128)(2,1)S(1)}, bf16[8,64,512]{2,1,0:T(8,128)(2,1)}, u32[]{:S(2)}) copy-start(bf16[8,64,512]{2,1,0:T(8,128)(2,1)} %get-tuple-element.5) | copy-start | bytes 1572868

commit v6 on v5

--- a/solution.py
+++ b/solution.py
@@ -294,12 +294,10 @@
             arrived(held2(mod4(x + 2), zz, chunk), x2s.at[zz, chunk])
             share2(mod4(x + 2), zz, chunk)
 
-    for part_of in (correlate_own, correlate_other):
-        def last(step, carry):
-            part_of(home(mod4(x + 2), step), step)
-            return carry
-
-        lax.fori_loop(0, 2, last, 0)
+    far_columns = [home(mod4(x + 2), half) for half in range(2)]
+    correlate_own(far_columns[0], 0)
+    correlate_other(far_columns[0], 0)
+    correlate_other(far_columns[1], 1)
 
     def weigh(number, target):
         half = k if number == 0 else 1 - k
@@ -315,6 +313,7 @@
     fetch.wait()
     weigh(1, gp)
     send(gp, gr, gs.at[0], partner)
+    correlate_own(far_columns[1], 1)
     weigh(0, go)
     arrived(z1p, k1s.at[0])
 

time: 112 us -> 112 us (level)
  no operation moved by 1% of the time
where the time goes in v6:
time: 112 us
  Pallas kernels  109 us (97%)
  local copies, waits for them, and re-layouts  2.02 us (2%)
    pallas_call x1, Pallas kernels, per_device(): pl.pallas_call(kernel, out_shape=[jax.ShapeDtypeStruct(cut, BF16)] * 2, i...  109 us

profile of v6, /device:TPU:0, one launch (start us, length us, event | category | flops | bytes accessed | tf_op | source)
XLA Modules:
  0.0 111.6 jit_solution(11016372909788469916)
XLA Ops:
  0.6 109.0 %shard_map.50 = (bf16[8,64,512]{2,1,0:T(8,128)(2,1)S(1)}, bf16[8,64,512]{2,1,0:T(8,128)(2,1)}) custom-call(bf16[8,64,512]{2,1,0:T(8,128)(2,1)} %bitcast.8, bf16[8,64,512]{2,1,0:T(8,128)(2,1)} %bitcast.9, bf16[2,512,512]{2,1,0:T(8,128)(2,1)} %bitcast.7), custom_call_target="tpu_custom_call" | custom-call | flops 12884901888 | bytes 2097152 | tf_op jit(solution)/shard_map/pallas_call | solution.py:482
  109.6 0.0 copy-start
  109.6 0.8 copy.7
  110.4 0.4 copy-done
  110.8 0.8 copy.8
Async XLA Ops:
  109.6 1.2 %copy-start = (bf16[8,64,512]{2,1,0:T(8,128)(2,1)S(1)}, bf16[8,64,512]{2,1,0:T(8,128)(2,1)}, u32[]{:S(2)}) copy-start(bf16[8,64,512]{2,1,0:T(8,128)(2,1)} %get-tuple-element.5) | copy-start | bytes 1572868
